TPU v7x, 8 devices: a whole 2x2x1 slice. The times are simulated.
8 devices in a mesh: dp: 2 (over z, y), row: 2 (over x), fsdp: 2 (over core).
Axes of the slice: x: 2, y: 2, z: 1, core: 2. Of those that a mesh axis runs over, the one named last changes fastest.
Arguments:
- x_in: bfloat16 [32768, 512], P(('dp', 'row', 'fsdp'))
- dy_out: bfloat16 [32768, 512], P(('dp', 'row', 'fsdp'))
- w_gate: bfloat16 [512, 1376], P(None, ('row', 'fsdp'))
- w_up: bfloat16 [512, 1376], P(None, ('row', 'fsdp'))
- w_down: bfloat16 [1376, 512], P(('row', 'fsdp'))
- g_next: float32 [8, 3, 512, 1376], P(('dp', 'row', 'fsdp'))
Outputs:
- output 1: bfloat16 [32768, 512], P(('dp', 'row', 'fsdp'))
- output 2: float32 [3, 512, 1376], P(None, None, ('row', 'fsdp'))
- output 3: float32 [8, 3, 512, 1376], P(('dp', 'row', 'fsdp'))
All inputs are finite; a program needn't handle non-finite values.
Results may differ from a plain program's by a relative error of at most 0.0108858.
Values are sent between devices in bfloat16 or wider.
A program may use at most 1 GiB of HBM per device.

v0:
```python
import jax
import jax.numpy as jnp
from jax import lax
from jax.sharding import PartitionSpec as P

GROUP_AXES = ("row", "fsdp")
ALL_AXES = ("dp", "row", "fsdp")
CONTRACT_LAST = (((1,), (1,)), ((), ()))
CONTRACT_FIRST = (((0,), (0,)), ((), ()))


def local_backward(x_blk, dy_blk, w_gate, w_up, w_down):
    a_pre = jnp.dot(x_blk, w_gate, preferred_element_type=jnp.float32)
    b_pre = jnp.dot(x_blk, w_up, preferred_element_type=jnp.float32)
    sig_a = jax.nn.sigmoid(a_pre)
    silu_a = a_pre * sig_a
    h_act = (silu_a * b_pre).astype(jnp.bfloat16)
    dh_full = lax.dot_general(dy_blk, w_down, CONTRACT_LAST, preferred_element_type=jnp.float32)
    da_bf = (dh_full * b_pre * sig_a * (1.0 + a_pre * (1.0 - sig_a))).astype(jnp.bfloat16)
    db_bf = (dh_full * silu_a).astype(jnp.bfloat16)
    dx_acc = lax.dot_general(da_bf, w_gate, CONTRACT_LAST, preferred_element_type=jnp.float32) + lax.dot_general(db_bf, w_up, CONTRACT_LAST, preferred_element_type=jnp.float32)
    grad_gate = lax.dot_general(x_blk, da_bf, CONTRACT_FIRST, preferred_element_type=jnp.float32)
    grad_up = lax.dot_general(x_blk, db_bf, CONTRACT_FIRST, preferred_element_type=jnp.float32)
    grad_down = lax.dot_general(dy_blk, h_act, CONTRACT_FIRST, preferred_element_type=jnp.float32)
    return dx_acc.astype(jnp.bfloat16), jnp.stack([grad_gate, grad_up, grad_down])


def solution(mesh):
    def per_device(x_blk, dy_blk, gate_shard, up_shard, down_shard, g_part):
        w_gate = lax.all_gather(gate_shard, GROUP_AXES, axis=1, tiled=True)
        w_up = lax.all_gather(up_shard, GROUP_AXES, axis=1, tiled=True)
        w_down = lax.all_gather(down_shard, GROUP_AXES, axis=0, tiled=True)
        dx_blk, dw_local = local_backward(x_blk, dy_blk, w_gate, w_up, w_down)
        g_summed = lax.psum(g_part[0].astype(jnp.bfloat16), "dp")
        g_shard = lax.psum_scatter(g_summed, GROUP_AXES, scatter_dimension=2, tiled=True)
        return dx_blk, g_shard.astype(jnp.float32), dw_local[None]

    return jax.shard_map(
        per_device,
        mesh=mesh,
        in_specs=(P(ALL_AXES, None), P(ALL_AXES, None), P(None, GROUP_AXES), P(None, GROUP_AXES), P(GROUP_AXES, None), P(ALL_AXES, None, None, None)),
        out_specs=(P(ALL_AXES, None), P(None, None, GROUP_AXES), P(ALL_AXES, None, None, None)),
        check_vma=False,
    )
```

profile of v0, /device:TPU:0, one launch (start us, length us, event | category | flops | bytes accessed | tf_op | source)
XLA Modules:
  0.0 243.0 jit_solution(10158045320874671691)
XLA Ops:
  7.2 0.0 copy-start.3
  7.2 0.0 all-reduce.6.cloned.1.call-start
  7.2 6.0 %convert_bitcast_fusion = bf16[3,512,1376]{1,2,0:T(8,128)(2,1)} fusion(f32[1,3,512,1376]{2,3,1,0:T(8,128)} %param.11), kind=kLoop, calls=%fused_computation.8 | loop fusion | flops 2113536 | bytes 12681216 | tf_op jit(solution)/shard_map/convert_element_type | solution.py:34
  13.2 0.0 all-reduce.6.cloned.1.call-update
  13.2 0.0 all-gather.6.cloned.1.call-start
  13.3 0.7 all-gather.6.cloned.1.call-update
  14.0 0.0 all-gather.8.cloned.1.call-start
  14.0 0.7 all-gather.8.cloned.1.call-update
  14.7 0.0 all-gather.4.cloned.1.call-start
  14.7 0.5 all-gather.4.cloned.1.call-update
  15.3 0.0 all-reduce.4.cloned.1.call-start
  15.3 0.0 copy-done.3
  15.3 0.6 dynamic-slice
  16.6 79.9 %all-reduce.6.cloned.1.call-done = bf16[3,512,1376]{1,2,0:T(8,128)(2,1)} async-done(((bf16[3,512,1376]{1,2,0:T(8,128)(2,1)}), bf16[3,512,1376]{1,2,0:T(8,128)(2,1)}) %all-reduce.6.cloned.1.call-update) | async-done | bytes 4227088
  96.5 2.3 constant_dynamic-slice_fusion
  98.8 0.0 all-reduce.4.cloned.1.call-update
  98.8 15.1 %all-gather.6.cloned.1.call-done = bf16[512,1376]{0,1:T(8,128)(2,1)} async-done(((bf16[512,344]{0,1:T(8,128)(2,1)}), bf16[512,1376]{0,1:T(8,128)(2,1)}) %all-gather.6.cloned.1.call-update) | async-done | bytes 1409040 | tf_op jit(solution)/shard_map/all_gather | solution.py:31
  113.9 12.6 %fusion.5 = f32[4096,1376]{0,1:T(8,128)} fusion(bf16[4096,512]{1,0:T(8,128)(2,1)} %param.6, bf16[512,1376]{0,1:T(8,128)(2,1)} %all-gather.6.cloned.1.call-done), kind=kOutput, calls=%fused_computation.14 | convolution fusion | flops 5771362304 | bytes 28147712 | tf_op jit(solution)/shard_map/dot_general | solution.py:14
  126.5 4.7 %all-gather.8.cloned.1.call-done = bf16[512,1376]{0,1:T(8,128)(2,1)} async-done(((bf16[512,344]{0,1:T(8,128)(2,1)}), bf16[512,1376]{0,1:T(8,128)(2,1)}) %all-gather.8.cloned.1.call-update) | async-done | bytes 1409040 | tf_op jit(solution)/shard_map/all_gather | solution.py:30
  131.2 12.6 %fusion.6 = f32[4096,1376]{0,1:T(8,128)} fusion(bf16[4096,512]{1,0:T(8,128)(2,1)} %param.6, bf16[512,1376]{0,1:T(8,128)(2,1)} %all-gather.8.cloned.1.call-done), kind=kOutput, calls=%fused_computation.15 | convolution fusion | flops 5771362304 | bytes 28147712 | tf_op jit(solution)/shard_map/dot_general | solution.py:13
  143.8 17.4 %fusion.3 = f32[1,512,1376]{1,2,0:T(8,128)S(1)} fusion(bf16[4096,512]{1,0:T(8,128)(2,1)} %param.7, f32[4096,1376]{0,1:T(8,128)} %fusion.5, f32[4096,1376]{0,1:T(8,128)} %fusion.6), kind=kOutput, calls=%fused_computation.9 | convolution fusion | flops 5805178880 | bytes 52101120 | tf_op jit(solution)/shard_map/dot_general | solution.py:24
  161.3 0.0 all-gather.4.cloned.1.call-done
  161.3 28.6 %multiply_convert_fusion.1 = (bf16[4096,1376]{0,1:T(8,128)(2,1)}, bf16[4096,1376]{0,1:T(8,128)(2,1)}) fusion(f32[4096,1376]{0,1:T(8,128)} %fusion.6, f32[4096,1376]{0,1:T(8,128)} %fusion.5, bf16[4096,512]{1,0:T(8,128)(2,1)} %param.7, bf16[1376,512]{1,0:T(8,128)(2,1)} %all-gather.4.cloned.1.call-done), kind=kOutput, calls=%fused_computation.1 | convolution fusion | flops 5844631552 | bytes 73236480 | tf_op jit(solution)/shard_map/dot_general | solution.py:18
  189.9 10.3 %convolution_bitcast_fusion = f32[1,512,1376]{1,2,0:T(8,128)S(1)} fusion(bf16[4096,1376]{0,1:T(8,128)(2,1)} %get-tuple-element.3, bf16[4096,512]{1,0:T(8,128)(2,1)} %param.6), kind=kOutput, calls=%fused_computation.10 | convolution fusion | flops 5771362304 | bytes 18284544 | tf_op jit(solution)/shard_map/dot_general | solution.py:23
  200.2 0.0 copy-done.2
  200.2 0.0 copy-done.4
  200.3 0.0 copy-start.1
  200.3 9.0 %fusion.7 = f32[4096,512]{1,0:T(8,128)} fusion(bf16[4096,1376]{0,1:T(8,128)(2,1)S(1)} %copy-done.4, bf16[512,1376]{0,1:T(8,128)(2,1)S(1)} %copy-done.2), kind=kOutput, calls=%fused_computation.16 | convolution fusion | flops 5771362304 | bytes 21069824 | tf_op jit(solution)/shard_map/dot_general | solution.py:21
  209.3 14.4 %add_convert_fusion = bf16[4096,512]{1,0:T(8,128)(2,1)} fusion(f32[4096,512]{1,0:T(8,128)} %fusion.7, bf16[4096,1376]{0,1:T(8,128)(2,1)} %get-tuple-element.3, bf16[512,1376]{0,1:T(8,128)(2,1)S(1)} %copy-done.1), kind=kOutput, calls=%fused_computation.7 | convolution fusion | flops 5775556608 | bytes 25264128 | tf_op jit(solution)/shard_map/dot_general | solution.py:21
  223.6 6.1 %convolution_bitcast_fusion.1 = f32[1,512,1376]{1,2,0:T(8,128)S(1)} fusion(bf16[4096,1376]{0,1:T(8,128)(2,1)S(1)} %copy-done.4, bf16[4096,512]{1,0:T(8,128)(2,1)S(1)} %copy-done), kind=kOutput, calls=%fused_computation.11 | convolution fusion | flops 5771362304 | bytes 18284544 | tf_op jit(solution)/shard_map/dot_general | solution.py:22
  229.8 3.9 %maximum_bitcast_fusion = f32[1,3,512,1376]{2,3,1,0:T(8,128)} fusion(f32[1,512,1376]{1,2,0:T(8,128)S(1)} %fusion.3, f32[1,512,1376]{1,2,0:T(8,128)S(1)} %convolution_bitcast_fusion, f32[1,512,1376]{1,2,0:T(8,128)S(1)} %convolution_bitcast_fusion.1), kind=kLoop, calls=%fused_computation.6 | loop fusion | flops 4227072 | bytes 16908288 | tf_op jit(solution)/shard_map/broadcast_in_dim | solution.py:36
  233.7 2.8 %convert_element_type.26 = f32[3,512,344]{1,2,0:T(8,128)} convert(bf16[3,512,344]{1,2,0:T(8,128)(2,1)} %all-reduce.4.cloned.1.call-done) | non-fusion elementwise | flops 528384 | bytes 3170304 | tf_op jit(solution)/shard_map/convert_element_type | solution.py:36
  (6 shorter events, 0.0 us)
Async XLA Ops:
  7.2 8.2 %copy-start.3 = (u32[8]{0:T(128)S(1)}, u32[8]{0:T(128)}, u32[]{:S(2)}) copy-start(u32[8]{0:T(128)} %constant.5) | copy-start | bytes 100
  7.2 89.3 %all-reduce.6.cloned.1.call-start = ((), (), s32[]{:S(2)}) async-start(), calls=%async_computation.4 | async-start | bytes 8454144
  13.2 100.7 %all-gather.6.cloned.1.call-start = ((), (), s32[]{:S(2)}) async-start(), calls=%async_computation.1 | async-start | bytes 1761280 | tf_op jit(solution)/shard_map/all_gather | solution.py:31
  14.0 117.2 %all-gather.8.cloned.1.call-start = ((), (), s32[]{:S(2)}) async-start(), calls=%async_computation.2 | async-start | bytes 1761280 | tf_op jit(solution)/shard_map/all_gather | solution.py:30
  14.7 146.6 %all-gather.4.cloned.1.call-start = ((), (), s32[]{:S(2)}) async-start(), calls=%async_computation | async-start | bytes 1761280 | tf_op jit(solution)/shard_map/all_gather | solution.py:32
  15.3 218.4 %all-reduce.4.cloned.1.call-start = ((), (), s32[]{:S(2)}) async-start(), calls=%async_computation.3 | async-start | bytes 2113536 | tf_op jit(solution)/shard_map/psum | solution.py:34
  189.9 10.4 %copy-start.2 = (bf16[512,1376]{0,1:T(8,128)(2,1)S(1)}, bf16[512,1376]{0,1:T(8,128)(2,1)}, u32[]{:S(2)}) copy-start(bf16[512,1376]{0,1:T(8,128)(2,1)} %all-gather.8.cloned.1.call-done) | copy-start | bytes 4227076
  189.9 10.4 %copy-start.4 = (bf16[4096,1376]{0,1:T(8,128)(2,1)S(1)}, bf16[4096,1376]{0,1:T(8,128)(2,1)}, u32[]{:S(2)}) copy-start(bf16[4096,1376]{0,1:T(8,128)(2,1)} %get-tuple-element.4) | copy-start | bytes 33816580
  200.3 9.0 %copy-start.1 = (bf16[512,1376]{0,1:T(8,128)(2,1)S(1)}, bf16[512,1376]{0,1:T(8,128)(2,1)}, u32[]{:S(2)}) copy-start(bf16[512,1376]{0,1:T(8,128)(2,1)} %all-gather.6.cloned.1.call-done) | copy-start | bytes 4227076
  209.3 14.4 %copy-start = (bf16[4096,512]{1,0:T(8,128)(2,1)S(1)}, bf16[4096,512]{1,0:T(8,128)(2,1)}, u32[]{:S(2)}) copy-start(bf16[4096,512]{1,0:T(8,128)(2,1)} %param.6) | copy-start | bytes 12582916
Sparse Core Ops, SparseCore 0:
  13.3 83.1 all-reduce.5
  98.0 15.8 all-gather.5
  115.5 15.7 all-gather.7
  132.6 15.7 all-gather.3
  151.1 34.4 all-reduce.3
where the time goes:
time: 243 us
  matrix products  111 us (46%)
  waiting for transfers between devices  102 us (42%)
  between operations  14.5 us (6%)
  other arithmetic  12.7 us (5%)
  local copies, waits for them, and re-layouts  2.87 us (1%)
    unnamed x6, waiting for transfers between devices  81.8 us
    dot_general x1, matrix products, local_backward(): lax.dot_general(dy_blk, w_down, CONTRACT_LAST, preferred_element_type=jnp...  28.6 us
    dot_general x1, matrix products, local_backward(): lax.dot_general(dy_blk, h_act, CONTRACT_FIRST, preferred_element_type=jnp...  17.4 us
    all_gather x1, waiting for transfers between devices, per_device(): w_up = lax.all_gather(up_shard, GROUP_AXES, axis=1, tiled=True)  15.1 us
    dot_general x1, matrix products, local_backward(): lax.dot_general(db_bf, w_up, CONTRACT_LAST, preferred_element_type=jnp.fl...  14.4 us
    dot_general x1, matrix products, local_backward(): b_pre = jnp.dot(x_blk, w_up, preferred_element_type=jnp.float32)  12.6 us
    dot_general x1, matrix products, local_backward(): a_pre = jnp.dot(x_blk, w_gate, preferred_element_type=jnp.float32)  12.6 us
    dot_general x1, matrix products, local_backward(): lax.dot_general(x_blk, db_bf, CONTRACT_FIRST, preferred_element_type=jnp....  10.3 us
  transfers between devices with their start and end apart: 5, of which 3 were waited for; matrix products, arithmetic and copies ran while one was open for 48% of the time, Pallas kernels for 0%

commit v1 on v0

v1 whole, which is shorter than its diff:
```python
import functools

import jax
import jax.numpy as jnp
from jax import lax
from jax.experimental import pallas as pl
from jax.experimental.pallas import tpu as pltpu
from jax.sharding import PartitionSpec as P

GROUP_AXES = ("row", "fsdp")
ALL_AXES = ("dp", "row", "fsdp")
MESH = pl.DeviceIdType.MESH
BF, F32 = jnp.bfloat16, jnp.float32

T, D, H = 4096, 512, 1376
HS = H // 4
HSP = 384
HQ = 2 * HSP
TB = 1024
NBLK = T // TB
NCH, CW = 6, 256
NWP, WW = 6, 128

NN = (((1,), (0,)), ((), ()))
NT = (((1,), (1,)), ((), ()))
TN = (((0,), (0,)), ((), ()))


def dot(a, b, dims):
    return lax.dot_general(a, b, dims, preferred_element_type=F32)


def gate_grads(a, b, dh):
    sig = 0.5 * jnp.tanh(0.5 * a) + 0.5
    silu = a * sig
    h = (silu * b).astype(BF)
    da = (dh * b * sig * (1.0 + a * (1.0 - sig))).astype(BF)
    db = (dh * silu).astype(BF)
    return h, da, db


def step_kernel(nb1, x_hbm, dy_hbm, w1_hbm, w3_hbm, w2_hbm, g_hbm, dx_hbm, dwt_hbm, gn_hbm,
                x, dy, wall, dxa, dxs, dab, dw, gst, pk, prec, xrec, yrec, gn,
                x_sem, dy_sem, ws_sem, g_sem, dx_sem, dw_sem, gn_sem,
                a1s, a1r, a2s, a2r, a3s, a3r, a4s, a4r, ps, pr, xs_, xr_, ys_, yr_):
    dp, row, f = (lax.axis_index(n) for n in ALL_AXES)
    partner, xn, yn = {"fsdp": 1 - f}, {"row": 1 - row}, {"dp": 1 - dp}
    mine = pl.ds(pl.multiple_of(f * HSP, HSP), HS)

    def xload(i):
        rows = pl.ds(pl.multiple_of(i * TB, TB), TB)
        return (pltpu.make_async_copy(x_hbm.at[rows], x.at[rows], x_sem.at[i]),
                pltpu.make_async_copy(dy_hbm.at[rows], dy.at[rows], dy_sem.at[i]))

    def gload(c):
        return pltpu.make_async_copy(g_hbm.at[c // 2, :, :, pl.ds((c % 2) * CW, CW)], gst.at[c % 3], g_sem.at[c % 3])

    def remote(src, dst, s, r, dev):
        return pltpu.make_async_remote_copy(src_ref=src, dst_ref=dst, send_sem=s, recv_sem=r, device_id=dev, device_id_type=MESH)

    def wload(m):
        return pltpu.make_async_copy((w1_hbm, w3_hbm, w2_hbm)[m], wall.at[0, m, mine], ws_sem.at[m])

    def a1(m):
        ref = wall.at[0, m, mine]
        return remote(ref, ref, a1s.at[m], a1r.at[m], partner)

    def piece(p, j, half):
        return wall.at[p, j // 2, mine, pl.ds(pl.multiple_of(half * 256 + (j % 2) * WW, WW), WW)]

    def a2(j):
        return remote(piece(0, j, dp), piece(1, j, dp), a2s.at[j], a2r.at[j], xn)

    def a3(j):
        ref = piece(1, j, dp)
        return remote(ref, ref, a3s.at[j], a3r.at[j], yn)

    def a4(n, j, half):
        ref = piece(1, j, half)
        return remote(ref, ref, a4s.at[n, j], a4r.at[n, j], partner)

    def psend(c):
        return remote(pk.at[c, 1 - f], prec.at[c], ps.at[c], pr.at[c], partner)

    def xsend(c):
        return remote(pk.at[c, f, 1 - row], xrec.at[c], xs_.at[c], xr_.at[c], xn)

    def ysend(c):
        return remote(pk.at[c, f, row], yrec.at[c], ys_.at[c], yr_.at[c], yn)

    edge = HS // 16 * 16
    for p in range(2):
        for m in range(3):
            for k in range(2):
                wall[p, m, k * HSP + edge:(k + 1) * HSP, :] = jnp.zeros((HSP - edge, D), BF)
    for m in range(3):
        wload(m).start()
    for c in range(3):
        gload(c).start()
    barrier = pltpu.get_barrier_semaphore()
    for dev in (partner, xn, yn):
        pl.semaphore_signal(barrier, inc=1, device_id=dev, device_id_type=MESH)
    pl.semaphore_wait(barrier, 3)
    for m in range(3):
        wload(m).wait()
        a1(m).start()
        a2(2 * m).start()
        a2(2 * m + 1).start()
    for cp in xload(0):
        cp.start()
    for c in range(NCH):
        gload(c).wait()
        for s in range(4):
            pk[c, s % 2, s // 2] = gst[c % 3, s].astype(BF)
        if c + 3 < NCH:
            gload(c + 3).start()
        if c > 0:
            psend(c - 1).start()
    for i in range(1, NBLK):
        for cp in xload(i):
            cp.start()
    psend(NCH - 1).start()
    for m in range(3):
        a1(m).wait_recv()

    def add1(c):
        psend(c).wait_recv()
        for k in range(2):
            pk[c, f, k] = (pk[c, f, k].astype(F32) + prec[c, k].astype(F32)).astype(BF)

    def add2(c):
        xsend(c).wait_recv()
        pk[c, f, row] = (pk[c, f, row].astype(F32) + xrec[c].astype(F32)).astype(BF)

    def fin(c):
        ysend(c).wait_recv()
        total = pk[c, f, row].astype(F32) + yrec[c].astype(F32)
        gn[c // 2, :, pl.ds(pl.multiple_of((c % 2) * CW, CW), CW)] = total

    def w_first(j):
        a2(j).wait_recv()
        a3(j).start()
        a4(0, j, dp).start()

    def w_second(j):
        a3(j).wait_recv()
        a4(1, j, 1 - dp).start()

    plan = [
        (2, 1, NWP, w_first),
        (4, 1, NWP, w_second),
        (2, 1, NCH, lambda c: xsend(c).start()),
        (1, 1, NCH, add1),
        (9, 2, NCH, lambda c: ysend(c).start()),
        (8, 2, NCH, add2),
        (12, 2, NCH, fin),
    ]

    def comm(q, lo, hi, sub):
        for first, stride, count, action in plan:
            last = first + stride * (count - 1)
            points = [n for n in range(first, last + 1, stride) if lo <= n < hi and n % 3 == sub]
            if points:
                ok = (q >= first) & (q <= last)
                if stride > 1:
                    ok = ok & ((q - first) % stride == 0)
                c = jnp.clip((q - first) // stride, 0, count - 1)
                pl.when(ok)(functools.partial(action, c))

    def run(p, nblocks):
        lo, hi = p * 3 * NBLK, p * 3 * NBLK + 3 * nblocks

        def body(i, carry):
            q = lo + 3 * i
            rows = pl.ds(pl.multiple_of(i * TB, TB), TB)
            if p == 0:
                for cp in xload(i):
                    cp.wait()
            else:
                slot = i % 2

                @pl.when(i >= 2)
                def _():
                    dx_out(i - 2).wait()
            comm(q, lo, hi, 0)
            xb, dyb = x[rows, :], dy[rows, :]
            a = dot(xb, wall[p, 0], NT)
            b = dot(xb, wall[p, 1], NT)
            dh = dot(dyb, wall[p, 2], NT)
            h, da, db = gate_grads(a, b, dh)
            dab[0], dab[1], dab[2] = da, db, h
            comm(q + 1, lo, hi, 1)
            r = dot(dab[0], wall[p, 0], NN) + dot(dab[1], wall[p, 1], NN)
            if p == 0:
                dxa[rows, :] = r
            else:
                dxs[slot] = (dxa[rows, :] + r).astype(BF)
            comm(q + 2, lo, hi, 2)
            if p == 1:
                dx_out(i).start()

                @pl.when(i == 0)
                def _():
                    dw_out(0).wait()
            xb, dyb = x[rows, :], dy[rows, :]
            for k in range(3):
                for s in range(2):
                    part = dot(dab[k, :, s * HSP:s * HSP + HS], dyb if k == 2 else xb, TN)
                    dw[k, s] = jnp.where(i == 0, 0.0, dw[k, s]) + part
            return carry

        lax.fori_loop(0, nblocks, body, 0)

    def dx_out(i):
        rows = pl.ds(pl.multiple_of(i * TB, TB), TB)
        return pltpu.make_async_copy(dxs.at[i % 2], dx_hbm.at[rows], dx_sem.at[i % 2])

    def dw_out(p):
        return pltpu.make_async_copy(dw, dwt_hbm.at[:, pl.ds(2 * (row if p == 0 else 1 - row), 2)], dw_sem)

    run(0, NBLK)
    dw_out(0).start()
    for j in range(NWP):
        a4(0, j, dp).wait_recv()
        a4(1, j, 1 - dp).wait_recv()
    run(1, nb1)
    dw_out(1).start()

    gn_copy = pltpu.make_async_copy(gn, gn_hbm, gn_sem)
    gn_copy.start()
    for m in range(3):
        a1(m).wait_send()
    for j in range(NWP):
        a2(j).wait_send()
        a3(j).wait_send()
        a4(0, j, dp).wait_send()
        a4(1, j, 1 - dp).wait_send()
    for c in range(NCH):
        psend(c).wait_send()
        xsend(c).wait_send()
        ysend(c).wait_send()
    dx_out(nb1 - 2).wait()
    dx_out(nb1 - 1).wait()
    dw_out(1).wait()
    gn_copy.wait()


def fused_step(x, dy, w1, w3, w2, g):
    any_space = pl.BlockSpec(memory_space=pl.ANY)
    dma = pltpu.SemaphoreType.DMA
    scratch = [
        pltpu.VMEM((T, D), BF), pltpu.VMEM((T, D), BF), pltpu.VMEM((2, 3, HQ, D), BF),
        pltpu.VMEM((T, D), F32), pltpu.VMEM((2, TB, D), BF), pltpu.VMEM((3, TB, HQ), BF), pltpu.VMEM((3, 2, HS, D), F32),
        pltpu.VMEM((3, 4, HS, CW), F32), pltpu.VMEM((NCH, 2, 2, HS, CW), BF), pltpu.VMEM((NCH, 2, HS, CW), BF),
        pltpu.VMEM((NCH, HS, CW), BF), pltpu.VMEM((NCH, HS, CW), BF), pltpu.VMEM((3, HS, D), F32),
        dma((NBLK,)), dma((NBLK,)), dma((3,)), dma((3,)), dma((2,)), dma, dma,
        dma((3,)), dma((3,)), dma((NWP,)), dma((NWP,)), dma((NWP,)), dma((NWP,)), dma((2, NWP)), dma((2, NWP)),
        dma((NCH,)), dma((NCH,)), dma((NCH,)), dma((NCH,)), dma((NCH,)), dma((NCH,)),
    ]
    return pl.pallas_call(
        functools.partial(step_kernel, NBLK),
        out_shape=(jax.ShapeDtypeStruct((T, D), BF), jax.ShapeDtypeStruct((3, 4, HS, D), F32), jax.ShapeDtypeStruct((3, HS, D), F32)),
        in_specs=[any_space] * 6,
        out_specs=(any_space,) * 3,
        scratch_shapes=scratch,
        compiler_params=pltpu.CompilerParams(collective_id=0, has_side_effects=True, vmem_limit_bytes=67043328),
    )(x, dy, w1, w3, w2, g)


def solution(mesh):
    def per_device(x_blk, dy_blk, gate_shard, up_shard, down_shard, g_part):
        g_t = jnp.swapaxes(g_part[0], 1, 2).reshape(3, 4, HS, D)
        dx_blk, dwt, gnt = fused_step(x_blk, dy_blk, gate_shard.T, up_shard.T, down_shard, g_t)
        dw_local = jnp.swapaxes(dwt.reshape(3, H, D), 1, 2)
        return dx_blk, jnp.swapaxes(gnt, 1, 2), dw_local[None]

    return jax.shard_map(
        per_device,
        mesh=mesh,
        in_specs=(P(ALL_AXES, None), P(ALL_AXES, None), P(None, GROUP_AXES), P(None, GROUP_AXES), P(GROUP_AXES, None), P(ALL_AXES, None, None, None)),
        out_specs=(P(ALL_AXES, None), P(None, None, GROUP_AXES), P(ALL_AXES, None, None, None)),
        check_vma=False,
    )
```

time: 243 us -> 86.6 us (0.36)
  matrix products: 111 us -> 0 us
  waiting for transfers between devices: 102 us -> 0 us
  Pallas kernels: 0 us -> 74.2 us
  between operations: 14.5 us -> 0.65 us
  other arithmetic: 12.7 us -> 0 us
  local copies, waits for them, and re-layouts: 2.87 us -> 11.7 us
    dot_general x8 -> x0, matrix products: 111 us -> none  [the longest x1 28.6 us: local_backward(): lax.dot_general(dy_blk, w_down, CONTRACT_LAST, preferred_element_type=jnp...]
    unnamed x6 -> x0, waiting for transfers between devices: 81.8 us -> none
    pallas_call x0 -> x1, Pallas kernels: none -> 74.2 us  [fused_step(): pl.pallas_call(functools.partial(step_kernel, NBLK), out_shape=(jax.Shape...]
    all_gather x3 -> x0, waiting for transfers between devices: 19.8 us -> none  [the longest x1 15.1 us: per_device(): w_up = lax.all_gather(up_shard, GROUP_AXES, axis=1, tiled=True)]
    convert_element_type x2 -> x0, other arithmetic: 8.81 us -> none  [the longest x1 5.97 us: per_device(): g_summed = lax.psum(g_part[0].astype(jnp.bfloat16), 'dp')]
    unnamed x12 -> x5, local copies, waits for them, and re-layouts: 2.87 us -> 11.7 us
    broadcast_in_dim x1 -> x0, other arithmetic: 3.88 us -> none  [per_device(): return (dx_blk, g_shard.astype(jnp.float32), dw_local[None])]
  transfers between devices with their start and end apart: 5 -> 0, of which waited for: 3 -> 0; matrix products, arithmetic and copies ran while one was open for 48% -> 0% of each run, Pallas kernels for 0% -> 0%
where the time goes in v1:
time: 86.6 us; the launch traced here: 86.5 us
  Pallas kernels  74.2 us (86%)
  local copies, waits for them, and re-layouts  11.7 us (14%)
    pallas_call x1, Pallas kernels, fused_step(): pl.pallas_call(functools.partial(step_kernel, NBLK), out_shape=(jax.Shape...  74.2 us
    unnamed x5, local copies, waits for them, and re-layouts  11.7 us

profile of v1, /device:TPU:0, one launch (start us, length us, event | category | flops | bytes accessed | tf_op | source)
XLA Modules:
  0.0 86.5 jit_solution(9313709081850701484)
XLA Ops:
  0.6 74.2 %shard_map.85 = (bf16[4096,512]{1,0:T(8,128)(2,1)}, f32[3,4,344,512]{3,2,1,0:T(8,128)}, f32[3,344,512]{2,1,0:T(8,128)}) custom-call(bf16[4096,512]{1,0:T(8,128)(2,1)} %x_hbm.1, bf16[4096,512]{1,0:T(8,128)(2,1)} %dy_hbm.1, bf16[344,512]{1,0:T(8,128)(2,1)} %bitcast.16, bf16[344,512]{1,0:T(8,128)(2,1)} %bitcast.17, bf16[344,512]{1,0:T(8,128)(2,1)} %w2_hbm.1, ...), custom_call_target="tpu_custom_call" | custom-call | tf_op jit(solution)/shard_map/pallas_call | solution.py:260
  74.8 0.0 copy-start
  74.8 4.8 %copy.12 = bf16[4096,512]{1,0:T(8,128)(2,1)} copy(bf16[4096,512]{1,0:T(8,128)(2,1)} %get-tuple-element.12) | data formatting | bytes 8388608
  79.6 3.5 %copy.13 = f32[3,512,344]{1,2,0:T(8,128)} copy(f32[3,512,344]{1,2,0:T(8,128)} %bitcast.15) | data formatting | bytes 4227072
  83.1 0.0 copy-done
  83.1 3.4 %copy.14 = f32[1,3,512,1376]{2,3,1,0:T(8,128)} copy(f32[1,3,512,1376]{2,3,1,0:T(8,128)S(1)} %bitcast.14) | data formatting | bytes 16908288
Async XLA Ops:
  74.8 8.3 %copy-start = (f32[3,4,344,512]{3,2,1,0:T(8,128)S(1)}, f32[3,4,344,512]{3,2,1,0:T(8,128)}, u32[]{:S(2)}) copy-start(f32[3,4,344,512]{3,2,1,0:T(8,128)} %get-tuple-element.8) | copy-start | bytes 25362436

commit v2 on v1

v2 whole, which is shorter than its diff:
```python
import functools

import jax
import jax.numpy as jnp
from jax import lax
from jax.experimental import pallas as pl
from jax.experimental.pallas import tpu as pltpu
from jax.sharding import PartitionSpec as P

GROUP_AXES = ("row", "fsdp")
ALL_AXES = ("dp", "row", "fsdp")
MESH = pl.DeviceIdType.MESH
BF, F32 = jnp.bfloat16, jnp.float32

T, D, H = 4096, 512, 1376
HS = H // 4
HSP = 384
HQ = 2 * HSP
TB = 1024
NBLK = T // TB
NCH, CW = 6, 256
NWP, WW = 6, 128
NT_COLS, GATE_ROWS = 256, 64
NB1 = 2

NN = (((1,), (0,)), ((), ()))
NT = (((1,), (1,)), ((), ()))
TN = (((0,), (0,)), ((), ()))


def dot(a, b, dims):
    return lax.dot_general(a, b, dims, preferred_element_type=F32)


def gate_grads(a, b, dh):
    sig = 0.5 * jnp.tanh(0.5 * a) + 0.5
    silu = a * sig
    h = (silu * b).astype(BF)
    da = (dh * b * sig * (1.0 + a * (1.0 - sig))).astype(BF)
    db = (dh * silu).astype(BF)
    return h, da, db


def block_rows(i):
    return pl.ds(i * TB if isinstance(i, int) else pl.multiple_of(i * TB, TB), TB)


def activations(xb, dyb, w, dab):
    for c in range(0, HQ, NT_COLS):
        cols = slice(c, c + NT_COLS)
        a = dot(xb, w[0, cols], NT)
        b = dot(xb, w[1, cols], NT)
        dh = dot(dyb, w[2, cols], NT)
        for r in range(0, TB, GATE_ROWS):
            rows = slice(r, r + GATE_ROWS)
            h, da, db = gate_grads(a[rows], b[rows], dh[rows])
            dab[0, rows, cols], dab[1, rows, cols], dab[2, rows, cols] = da, db, h


def input_grad(w, dab):
    return dot(dab[0], w[0], NN) + dot(dab[1], w[1], NN)


def weight_grad(k, xb, dyb, dab, dw, fresh):
    for s in range(2):
        part = dot(dab[k, :, s * HSP:s * HSP + HS], dyb if k == 2 else xb, TN)
        if fresh is True:
            dw[k, s] = part
        elif fresh is False:
            dw[k, s] = dw[k, s] + part
        else:
            dw[k, s] = jnp.where(fresh, 0.0, dw[k, s]) + part


def first_kernel(x_hbm, dy_hbm, w1_hbm, w3_hbm, w2_hbm, g_hbm,
                 dxr_hbm, dxa_hbm, dw0_hbm, dwa_hbm, w_hbm, gp_hbm, gy_hbm,
                 x, dy, wall, dxa, dxs, dab, dw, gst, pk, prec, xrec,
                 x_sem, dy_sem, ws_sem, g_sem, dx_sem, dxa_sem, dw0_sem, dwa_sem, w_sem, gp_sem,
                 a1s, a1r, a2s, a2r, a3s, a3r, a4s, a4r, ps, pr, xs_, xr_, ys_, yr_):
    dp, row, f = (lax.axis_index(n) for n in ALL_AXES)
    partner, xn, yn = {"fsdp": 1 - f}, {"row": 1 - row}, {"dp": 1 - dp}
    mine = pl.ds(pl.multiple_of(f * HSP, HSP), HS)

    def xload(i):
        rows = block_rows(i)
        return (pltpu.make_async_copy(x_hbm.at[rows], x.at[rows], x_sem.at[i]),
                pltpu.make_async_copy(dy_hbm.at[rows], dy.at[rows], dy_sem.at[i]))

    def gload(c):
        return pltpu.make_async_copy(g_hbm.at[c // 2, :, :, pl.ds((c % 2) * CW, CW)], gst.at[c % 3], g_sem.at[c % 3])

    def remote(src, dst, s, r, dev):
        return pltpu.make_async_remote_copy(src_ref=src, dst_ref=dst, send_sem=s, recv_sem=r, device_id=dev, device_id_type=MESH)

    def wload(m):
        return pltpu.make_async_copy((w1_hbm, w3_hbm, w2_hbm)[m], wall.at[0, m, mine], ws_sem.at[m])

    def a1(m):
        ref = wall.at[0, m, mine]
        return remote(ref, ref, a1s.at[m], a1r.at[m], partner)

    def piece(p, j, half):
        return wall.at[p, j // 2, mine, pl.ds(pl.multiple_of(half * 256 + (j % 2) * WW, WW), WW)]

    def a2(j):
        return remote(piece(0, j, dp), piece(1, j, dp), a2s.at[j], a2r.at[j], xn)

    def a3(j):
        ref = piece(1, j, dp)
        return remote(ref, ref, a3s.at[j], a3r.at[j], yn)

    def a4(n, j, half):
        ref = piece(1, j, half)
        return remote(ref, ref, a4s.at[n, j], a4r.at[n, j], partner)

    def psend(c):
        return remote(pk.at[c, 1 - f], prec.at[c], ps.at[c], pr.at[c], partner)

    def xsend(c):
        return remote(pk.at[c, f, 1 - row], xrec.at[c], xs_.at[c], xr_.at[c], xn)

    def ysend(c):
        return remote(pk.at[c, f, row], gy_hbm.at[c], ys_.at[c], yr_.at[c], yn)

    def gp_out(c):
        return pltpu.make_async_copy(pk.at[c, f, row], gp_hbm.at[c], gp_sem.at[c])

    def dx_out(i):
        return pltpu.make_async_copy(dxs.at[i % 2], dxr_hbm.at[block_rows(i)], dx_sem.at[i % 2])

    def dwa_out(k):
        return pltpu.make_async_copy(dw.at[k], dwa_hbm.at[k], dwa_sem.at[k])

    dw0_out = pltpu.make_async_copy(dw, dw0_hbm, dw0_sem)
    dxa_out = pltpu.make_async_copy(dxa.at[pl.ds(NB1 * TB, T - NB1 * TB)], dxa_hbm, dxa_sem)
    w_out = pltpu.make_async_copy(wall.at[1], w_hbm, w_sem)

    def convert(c):
        gload(c).wait()
        for s in range(4):
            pk[c, s % 2, s // 2] = gst[c % 3, s].astype(BF)

    edge = HS // 16 * 16
    for p in range(2):
        for m in range(3):
            for k in range(2):
                wall[p, m, k * HSP + edge:(k + 1) * HSP, :] = jnp.zeros((HSP - edge, D), BF)
    for m in range(3):
        wload(m).start()
    for c in range(2):
        gload(c).start()
    for cp in xload(0):
        cp.start()
    gload(2).start()
    barrier = pltpu.get_barrier_semaphore()
    for dev in (partner, xn, yn):
        pl.semaphore_signal(barrier, inc=1, device_id=dev, device_id_type=MESH)
    pl.semaphore_wait(barrier, 3)
    for m in range(3):
        wload(m).wait()
        a1(m).start()
        a2(2 * m).start()
        a2(2 * m + 1).start()
    for c in range(2):
        convert(c)
        gload(c + 3).start()
    for i in range(1, NBLK):
        for cp in xload(i):
            cp.start()
    for c in range(2):
        psend(c).start()
    for m in range(3):
        a1(m).wait_recv()

    def add1(c):
        psend(c).wait_recv()
        for k in range(2):
            pk[c, f, k] = (pk[c, f, k].astype(F32) + prec[c, k].astype(F32)).astype(BF)

    def add2(c):
        xsend(c).wait_recv()
        pk[c, f, row] = (pk[c, f, row].astype(F32) + xrec[c].astype(F32)).astype(BF)

    def w_first(j):
        a2(j).wait_recv()
        a3(j).start()
        a4(0, j, dp).start()

    def w_second(j):
        a3(j).wait_recv()
        a4(1, j, 1 - dp).start()

    plan = {
        1: ((0,), (), (2, 3, 4), (), ()),
        2: ((1, 2), (), (5,), (0, 1), ()),
        3: ((3,), (0,), (), (2, 3, 4), ()),
        4: ((4, 5), (1,), (), (5,), ()),
        5: ((), (2, 3), (), (), (0,)),
        6: ((), (4, 5), (), (), (1,)),
        7: ((), (), (), (), (2,)),
        8: ((), (), (), (), (3,)),
        10: ((), (), (), (), (4,)),
        11: ((), (), (), (), (5,)),
    }

    def actions(n):
        first, second, conv, chip, over_x = plan[n]
        for j in first:
            w_first(j)
        for j in second:
            w_second(j)
        for c in conv:
            convert(c)
            if c + 3 < NCH:
                gload(c + 3).start()
        for c in chip:
            add1(c)
        for c in over_x:
            add2(c)
        for c in conv:
            psend(c).start()
        for c in chip:
            xsend(c).start()
        for c in over_x:
            ysend(c).start()
            gp_out(c).start()

    def body(i, carry):
        rows = block_rows(i)
        for cp in xload(i):
            cp.wait()
        for blk in range(NBLK):
            if 2 * blk in plan:
                pl.when(i == blk)(functools.partial(actions, 2 * blk))
        activations(x[rows, :], dy[rows, :], wall.at[0], dab)
        for blk in range(NBLK):
            if 2 * blk + 1 in plan:
                pl.when(i == blk)(functools.partial(actions, 2 * blk + 1))
        dxa[rows, :] = input_grad(wall.at[0], dab)
        for k in range(3):
            weight_grad(k, x[rows, :], dy[rows, :], dab, dw, i == 0)
        return carry

    lax.fori_loop(0, NBLK, body, 0)
    dw0_out.start()
    dxa_out.start()
    for j in range(NWP):
        a4(0, j, dp).wait_recv()
        a4(1, j, 1 - dp).wait_recv()
    w_out.start()

    for i in range(NB1):
        rows = block_rows(i)
        n = 2 * (NBLK + i)
        if n in plan:
            actions(n)
        activations(x[rows, :], dy[rows, :], wall.at[1], dab)
        if n + 1 in plan:
            actions(n + 1)
        dxs[i % 2] = (dxa[rows, :] + input_grad(wall.at[1], dab)).astype(BF)
        if i == 0:
            dw0_out.wait()
        for k in range(3):
            weight_grad(k, x[rows, :], dy[rows, :], dab, dw, i == 0)
            if i == NB1 - 1:
                dwa_out(k).start()
        dx_out(i).start()

    for m in range(3):
        a1(m).wait_send()
    for j in range(NWP):
        a2(j).wait_send()
        a3(j).wait_send()
        a4(0, j, dp).wait_send()
        a4(1, j, 1 - dp).wait_send()
    for c in range(NCH):
        psend(c).wait_send()
        xsend(c).wait_send()
        ysend(c).wait_send()
        gp_out(c).wait()
    for i in range(NB1):
        dx_out(i).wait()
    dxa_out.wait()
    w_out.wait()
    for k in range(3):
        dwa_out(k).wait()
    for c in range(NCH):
        ysend(c).wait_recv()


def second_kernel(x_hbm, dy_hbm, dxr_hbm, dxa_hbm, dw0_hbm, dwa_hbm, w_hbm, gp_hbm, gy_hbm,
                  dx_hbm, dwt_hbm, gn_hbm,
                  x, dy, w, dxr, dxa, dxs, dab, dw, dw0, gp, gy, gn,
                  x_sem, dy_sem, w_sem, dxa_sem, in_sem, dx_sem, dw_sem, out_sem):
    row = lax.axis_index("row")
    nb = NBLK - NB1

    def xload(i):
        rows = block_rows(NB1 + i)
        return (pltpu.make_async_copy(x_hbm.at[rows], x.at[i], x_sem.at[i]),
                pltpu.make_async_copy(dy_hbm.at[rows], dy.at[i], dy_sem.at[i]),
                pltpu.make_async_copy(dxa_hbm.at[block_rows(i)], dxa.at[i], dxa_sem.at[i]))

    def dx_out(i):
        return pltpu.make_async_copy(dxs.at[i], dx_hbm.at[block_rows(NB1 + i)], dx_sem.at[i])

    def dw_out(k):
        return pltpu.make_async_copy(dw.at[k], dwt_hbm.at[k, pl.ds(2 * (1 - row), 2)], dw_sem.at[k])

    w_in = pltpu.make_async_copy(w_hbm, w, w_sem)
    dwa_in, gp_in, gy_in, dxr_in, dw0_in = (
        pltpu.make_async_copy(src, dst, in_sem.at[n])
        for n, (src, dst) in enumerate([(dwa_hbm, dw), (gp_hbm, gp), (gy_hbm, gy), (dxr_hbm, dxr), (dw0_hbm, dw0)]))
    dxr_out = pltpu.make_async_copy(dxr, dx_hbm.at[pl.ds(0, NB1 * TB)], out_sem.at[0])
    dw0_out = pltpu.make_async_copy(dw0, dwt_hbm.at[:, pl.ds(2 * row, 2)], out_sem.at[1])
    gn_out = pltpu.make_async_copy(gn, gn_hbm, out_sem.at[2])

    w_in.start()
    for cp in xload(0):
        cp.start()
    dwa_in.start()
    for i in range(1, nb):
        for cp in xload(i):
            cp.start()
    for cp in (gp_in, gy_in, dxr_in, dw0_in):
        cp.start()
    w_in.wait()
    for i in range(nb):
        for cp in xload(i):
            cp.wait()
        activations(x[i], dy[i], w, dab)
        if i == 0:
            dwa_in.wait()
        else:
            dxr_in.wait()
            dxr_out.start()
            dw0_in.wait()
            dw0_out.start()
            gp_in.wait()
            gy_in.wait()
            for c in range(NCH):
                gn[c // 2, :, (c % 2) * CW:(c % 2 + 1) * CW] = gp[c].astype(F32) + gy[c].astype(F32)
        dxs[i] = (dxa[i] + input_grad(w, dab)).astype(BF)
        for k in range(3):
            weight_grad(k, x[i], dy[i], dab, dw, False)
            if i == nb - 1:
                dw_out(k).start()
        dx_out(i).start()
        if i == nb - 1:
            gn_out.start()
    for i in range(nb):
        dx_out(i).wait()
    for k in range(3):
        dw_out(k).wait()
    for cp in (dxr_out, dw0_out, gn_out):
        cp.wait()


def fused_step(x, dy, w1, w3, w2, g):
    any_space = pl.BlockSpec(memory_space=pl.ANY)
    dma = pltpu.SemaphoreType.DMA
    vmem = pltpu.VMEM
    sds = jax.ShapeDtypeStruct
    nb = NBLK - NB1
    scratch = [
        vmem((T, D), BF), vmem((T, D), BF), vmem((2, 3, HQ, D), BF),
        vmem((T, D), F32), vmem((2, TB, D), BF), vmem((3, TB, HQ), BF), vmem((3, 2, HS, D), F32),
        vmem((3, 4, HS, CW), F32), vmem((NCH, 2, 2, HS, CW), BF), vmem((NCH, 2, HS, CW), BF), vmem((NCH, HS, CW), BF),
        dma((NBLK,)), dma((NBLK,)), dma((3,)), dma((3,)), dma((2,)), dma, dma, dma((3,)), dma, dma((NCH,)),
        dma((3,)), dma((3,)), dma((NWP,)), dma((NWP,)), dma((NWP,)), dma((NWP,)), dma((2, NWP)), dma((2, NWP)),
        dma((NCH,)), dma((NCH,)), dma((NCH,)), dma((NCH,)), dma((NCH,)), dma((NCH,)),
    ]
    part = sds((3, 2, HS, D), F32)
    chunks = sds((NCH, HS, CW), BF)
    carried = pl.pallas_call(
        first_kernel,
        out_shape=(sds((NB1 * TB, D), BF), sds((nb * TB, D), F32), part, part, sds((3, HQ, D), BF), chunks, chunks),
        in_specs=[any_space] * 6,
        out_specs=(any_space,) * 7,
        scratch_shapes=scratch,
        compiler_params=pltpu.CompilerParams(collective_id=0, has_side_effects=True, vmem_limit_bytes=67043328),
    )(x, dy, w1, w3, w2, g)
    scratch = [
        vmem((nb, TB, D), BF), vmem((nb, TB, D), BF), vmem((3, HQ, D), BF), vmem((NB1 * TB, D), BF), vmem((nb, TB, D), F32),
        vmem((nb, TB, D), BF), vmem((3, TB, HQ), BF), vmem((3, 2, HS, D), F32), vmem((3, 2, HS, D), F32),
        vmem((NCH, HS, CW), BF), vmem((NCH, HS, CW), BF), vmem((3, HS, D), F32),
        dma((nb,)), dma((nb,)), dma, dma((nb,)), dma((5,)), dma((nb,)), dma((3,)), dma((3,)),
    ]
    return pl.pallas_call(
        second_kernel,
        out_shape=(sds((T, D), BF), sds((3, 4, HS, D), F32), sds((3, HS, D), F32)),
        in_specs=[any_space] * 9,
        out_specs=(any_space,) * 3,
        scratch_shapes=scratch,
        compiler_params=pltpu.CompilerParams(vmem_limit_bytes=67043328),
    )(x, dy, *carried)


def solution(mesh):
    def per_device(x_blk, dy_blk, gate_shard, up_shard, down_shard, g_part):
        g_t = jnp.swapaxes(g_part[0], 1, 2).reshape(3, 4, HS, D)
        dx_blk, dwt, gnt = fused_step(x_blk, dy_blk, gate_shard.T, up_shard.T, down_shard, g_t)
        dw_local = jnp.swapaxes(dwt.reshape(3, H, D), 1, 2)
        return dx_blk, jnp.swapaxes(gnt, 1, 2), dw_local[None]

    return jax.shard_map(
        per_device,
        mesh=mesh,
        in_specs=(P(ALL_AXES, None), P(ALL_AXES, None), P(None, GROUP_AXES), P(None, GROUP_AXES), P(GROUP_AXES, None), P(ALL_AXES, None, None, None)),
        out_specs=(P(ALL_AXES, None), P(None, None, GROUP_AXES), P(ALL_AXES, None, None, None)),
        check_vma=False,
    )
```

time: 86.6 us -> 79.4 us (0.917)
  local copies, waits for them, and re-layouts: 11.7 us -> 0 us
  Pallas kernels: 74.2 us -> 78.5 us
    unnamed x5 -> x0, local copies, waits for them, and re-layouts: 11.7 us -> none
    pallas_call x1 -> x2, Pallas kernels: 74.2 us -> 78.5 us  [the longest x1 56.5 us: fused_step(): pl.pallas_call(first_kernel, out_shape=(sds((NB1 * TB, D), BF), sds((nb *...]
where the time goes in v2:
time: 79.4 us; the launch traced here: 79.3 us
  Pallas kernels  78.5 us (99%)
  between operations  0.82 us (1%)
    pallas_call x1, Pallas kernels, fused_step(): pl.pallas_call(first_kernel, out_shape=(sds((NB1 * TB, D), BF), sds((nb *...  56.5 us
    pallas_call x1, Pallas kernels, fused_step(): pl.pallas_call(second_kernel, out_shape=(sds((T, D), BF), sds((3, 4, HS,...  22 us

profile of v2, /device:TPU:0, one launch (start us, length us, event | category | flops | bytes accessed | tf_op | source)
XLA Modules:
  0.0 79.3 jit_solution(3616777253635763612)
XLA Ops:
  0.6 56.5 %shard_map.85 = (bf16[2048,512]{1,0:T(8,128)(2,1)}, f32[2048,512]{1,0:T(8,128)}, f32[3,2,344,512]{3,2,1,0:T(8,128)}, f32[3,2,344,512]{3,2,1,0:T(8,128)}, bf16[3,...) custom-call(bf16[4096,512]{1,0:T(8,128)(2,1)} %x_hbm.3, ...), custom_call_target="tpu_custom_call" | custom-call | tf_op jit(solution)/shard_map/pallas_call | solution.py:375
  57.1 22.0 %shard_map.86 = (bf16[4096,512]{1,0:T(8,128)(2,1)}, f32[3,4,344,512]{3,2,1,0:T(8,128)}, f32[3,344,512]{2,1,0:T(8,128)}) custom-call(bf16[4096,512]{1,0:T(8,128)(2,1)} %x_hbm.3, bf16[4096,512]{1,0:T(8,128)(2,1)} %dy_hbm.3, bf16[2048,512]{1,0:T(8,128)(2,1)} %get-tuple-element.13.dxr_hbm, f32[2048,512]{1,0:T(8,128)} %get-tuple-element.14.dxa_hbm, ...), custom_call_target="tpu_custom_call" | custom-call | tf_op jit(solution)/shard_map/pallas_call | solution.py:389

commit v3 on v2

--- a/solution.py
+++ b/solution.py
@@ -191,16 +191,11 @@
         a4(1, j, 1 - dp).start()
 
     plan = {
-        1: ((0,), (), (2, 3, 4), (), ()),
-        2: ((1, 2), (), (5,), (0, 1), ()),
-        3: ((3,), (0,), (), (2, 3, 4), ()),
-        4: ((4, 5), (1,), (), (5,), ()),
-        5: ((), (2, 3), (), (), (0,)),
-        6: ((), (4, 5), (), (), (1,)),
-        7: ((), (), (), (), (2,)),
-        8: ((), (), (), (), (3,)),
-        10: ((), (), (), (), (4,)),
-        11: ((), (), (), (), (5,)),
+        2: ((0, 1, 2, 3), (), (2, 3, 4), (0, 1), ()),
+        4: ((4, 5), (), (5,), (2, 3, 4), (0,)),
+        6: ((), (0, 1, 2, 3, 4, 5), (), (5,), (1, 2)),
+        8: ((), (), (), (), (3, 4)),
+        9: ((), (), (), (), (5,)),
     }
 
     def actions(n):
@@ -233,9 +228,6 @@
             if 2 * blk in plan:
                 pl.when(i == blk)(functools.partial(actions, 2 * blk))
         activations(x[rows, :], dy[rows, :], wall.at[0], dab)
-        for blk in range(NBLK):
-            if 2 * blk + 1 in plan:
-                pl.when(i == blk)(functools.partial(actions, 2 * blk + 1))
         dxa[rows, :] = input_grad(wall.at[0], dab)
         for k in range(3):
             weight_grad(k, x[rows, :], dy[rows, :], dab, dw, i == 0)
@@ -257,13 +249,13 @@
         activations(x[rows, :], dy[rows, :], wall.at[1], dab)
         if n + 1 in plan:
             actions(n + 1)
-        dxs[i % 2] = (dxa[rows, :] + input_grad(wall.at[1], dab)).astype(BF)
         if i == 0:
             dw0_out.wait()
         for k in range(3):
             weight_grad(k, x[rows, :], dy[rows, :], dab, dw, i == 0)
             if i == NB1 - 1:
                 dwa_out(k).start()
+        dxs[i % 2] = (dxa[rows, :] + input_grad(wall.at[1], dab)).astype(BF)
         dx_out(i).start()
 
     for m in range(3):
@@ -316,9 +308,10 @@
     gn_out = pltpu.make_async_copy(gn, gn_hbm, out_sem.at[2])
 
     w_in.start()
-    for cp in xload(0):
+    for cp in xload(0)[:2]:
         cp.start()
     dwa_in.start()
+    xload(0)[2].start()
     for i in range(1, nb):
         for cp in xload(i):
             cp.start()
@@ -326,12 +319,20 @@
         cp.start()
     w_in.wait()
     for i in range(nb):
-        for cp in xload(i):
-            cp.wait()
+        x_in, dy_in, dxa_in = xload(i)
+        x_in.wait()
+        dy_in.wait()
         activations(x[i], dy[i], w, dab)
         if i == 0:
             dwa_in.wait()
-        else:
+        for k in range(3):
+            weight_grad(k, x[i], dy[i], dab, dw, False)
+            if i == nb - 1:
+                dw_out(k).start()
+        dxa_in.wait()
+        dxs[i] = (dxa[i] + input_grad(w, dab)).astype(BF)
+        dx_out(i).start()
+        if i == 0:
             dxr_in.wait()
             dxr_out.start()
             dw0_in.wait()
@@ -340,13 +341,6 @@
             gy_in.wait()
             for c in range(NCH):
                 gn[c // 2, :, (c % 2) * CW:(c % 2 + 1) * CW] = gp[c].astype(F32) + gy[c].astype(F32)
-        dxs[i] = (dxa[i] + input_grad(w, dab)).astype(BF)
-        for k in range(3):
-            weight_grad(k, x[i], dy[i], dab, dw, False)
-            if i == nb - 1:
-                dw_out(k).start()
-        dx_out(i).start()
-        if i == nb - 1:
             gn_out.start()
     for i in range(nb):
         dx_out(i).wait()

time: 79.4 us -> 75.8 us (0.955)
  Pallas kernels: 78.5 us -> 74.8 us
    pallas_call x1, Pallas kernels: 56.5 us -> 53.4 us  [fused_step(): pl.pallas_call(first_kernel, out_shape=(sds((NB1 * TB, D), BF), sds((nb *...]
where the time goes in v3:
time: 75.8 us; the launch traced here: 75.7 us
  Pallas kernels  74.8 us (99%)
  between operations  0.82 us (1%)
    pallas_call x1, Pallas kernels, fused_step(): pl.pallas_call(first_kernel, out_shape=(sds((NB1 * TB, D), BF), sds((nb *...  53.4 us
    pallas_call x1, Pallas kernels, fused_step(): pl.pallas_call(second_kernel, out_shape=(sds((T, D), BF), sds((3, 4, HS,...  21.5 us

profile of v3, /device:TPU:0, one launch (start us, length us, event | category | flops | bytes accessed | tf_op | source)
XLA Modules:
  0.0 75.7 jit_solution(959714811204202289)
XLA Ops:
  0.6 53.4 %shard_map.85 = (bf16[2048,512]{1,0:T(8,128)(2,1)}, f32[2048,512]{1,0:T(8,128)}, f32[3,2,344,512]{3,2,1,0:T(8,128)}, f32[3,2,344,512]{3,2,1,0:T(8,128)}, bf16[3,...) custom-call(bf16[4096,512]{1,0:T(8,128)(2,1)} %x_hbm.3, ...), custom_call_target="tpu_custom_call" | custom-call | tf_op jit(solution)/shard_map/pallas_call | solution.py:369
  54.0 21.5 %shard_map.86 = (bf16[4096,512]{1,0:T(8,128)(2,1)}, f32[3,4,344,512]{3,2,1,0:T(8,128)}, f32[3,344,512]{2,1,0:T(8,128)}) custom-call(bf16[4096,512]{1,0:T(8,128)(2,1)} %x_hbm.3, bf16[4096,512]{1,0:T(8,128)(2,1)} %dy_hbm.3, bf16[2048,512]{1,0:T(8,128)(2,1)} %get-tuple-element.13.dxr_hbm, f32[2048,512]{1,0:T(8,128)} %get-tuple-element.14.dxa_hbm, ...), custom_call_target="tpu_custom_call" | custom-call | tf_op jit(solution)/shard_map/pallas_call | solution.py:383

commit v4 on v3

--- a/solution.py
+++ b/solution.py
@@ -45,8 +45,9 @@
     return pl.ds(i * TB if isinstance(i, int) else pl.multiple_of(i * TB, TB), TB)
 
 
-def activations(xb, dyb, w, dab):
+def activations(xb, dyb, w, dab, before=lambda tile: None):
     for c in range(0, HQ, NT_COLS):
+        before(c // NT_COLS)
         cols = slice(c, c + NT_COLS)
         a = dot(xb, w[0, cols], NT)
         b = dot(xb, w[1, cols], NT)
@@ -147,11 +148,6 @@
                 wall[p, m, k * HSP + edge:(k + 1) * HSP, :] = jnp.zeros((HSP - edge, D), BF)
     for m in range(3):
         wload(m).start()
-    for c in range(2):
-        gload(c).start()
-    for cp in xload(0):
-        cp.start()
-    gload(2).start()
     barrier = pltpu.get_barrier_semaphore()
     for dev in (partner, xn, yn):
         pl.semaphore_signal(barrier, inc=1, device_id=dev, device_id_type=MESH)
@@ -161,16 +157,21 @@
         a1(m).start()
         a2(2 * m).start()
         a2(2 * m + 1).start()
+    for cp in xload(0):
+        cp.start()
+    for c in range(2):
+        gload(c).start()
     for c in range(2):
         convert(c)
-        gload(c + 3).start()
-    for i in range(1, NBLK):
-        for cp in xload(i):
-            cp.start()
     for c in range(2):
         psend(c).start()
     for m in range(3):
         a1(m).wait_recv()
+    for c in range(2, 5):
+        gload(c).start()
+    for i in range(1, NBLK):
+        for cp in xload(i):
+            cp.start()
 
     def add1(c):
         psend(c).wait_recv()
@@ -206,7 +207,7 @@
             w_second(j)
         for c in conv:
             convert(c)
-            if c + 3 < NCH:
+            if 5 <= c + 3 < NCH:
                 gload(c + 3).start()
         for c in chip:
             add1(c)
@@ -299,7 +300,10 @@
     def dw_out(k):
         return pltpu.make_async_copy(dw.at[k], dwt_hbm.at[k, pl.ds(2 * (1 - row), 2)], dw_sem.at[k])
 
-    w_in = pltpu.make_async_copy(w_hbm, w, w_sem)
+    def w_in(t):
+        rows = pl.ds(t * NT_COLS, NT_COLS)
+        return pltpu.make_async_copy(w_hbm.at[:, rows], w.at[:, rows], w_sem.at[t])
+
     dwa_in, gp_in, gy_in, dxr_in, dw0_in = (
         pltpu.make_async_copy(src, dst, in_sem.at[n])
         for n, (src, dst) in enumerate([(dwa_hbm, dw), (gp_hbm, gp), (gy_hbm, gy), (dxr_hbm, dxr), (dw0_hbm, dw0)]))
@@ -307,29 +311,51 @@
     dw0_out = pltpu.make_async_copy(dw0, dwt_hbm.at[:, pl.ds(2 * row, 2)], out_sem.at[1])
     gn_out = pltpu.make_async_copy(gn, gn_hbm, out_sem.at[2])
 
-    w_in.start()
-    for cp in xload(0)[:2]:
-        cp.start()
-    dwa_in.start()
-    xload(0)[2].start()
-    for i in range(1, nb):
-        for cp in xload(i):
-            cp.start()
-    for cp in (gp_in, gy_in, dxr_in, dw0_in):
-        cp.start()
-    w_in.wait()
+    tiles = HQ // NT_COLS
+    x_in, dy_in, dxa_in = zip(*[xload(i) for i in range(nb)])
+    w_in(0).start()
+    x_in[0].start()
+    dy_in[0].start()
+    for t in range(1, tiles):
+        w_in(t).start()
+    x_in[0].wait()
+    dy_in[0].wait()
     for i in range(nb):
-        x_in, dy_in, dxa_in = xload(i)
-        x_in.wait()
-        dy_in.wait()
-        activations(x[i], dy[i], w, dab)
+        last = i == nb - 1
+        if i > 0:
+            x_in[i].wait()
+            dy_in[i].wait()
+
+        def before(t):
+            if i == 0:
+                w_in(t).wait()
+                if t == tiles - 1:
+                    dwa_in.start()
+                    dxa_in[0].start()
+
+        activations(x[i], dy[i], w, dab, before)
         if i == 0:
             dwa_in.wait()
+        if not last:
+            for cp in (x_in[i + 1], dy_in[i + 1], dxa_in[i + 1]):
+                cp.start()
+        if i == 0:
+            dxr_in.start()
+            dw0_in.start()
+        if last:
+            gp_in.wait()
+            gy_in.wait()
+            for c in range(NCH):
+                gn[c // 2, :, (c % 2) * CW:(c % 2 + 1) * CW] = gp[c].astype(F32) + gy[c].astype(F32)
+            gn_out.start()
         for k in range(3):
             weight_grad(k, x[i], dy[i], dab, dw, False)
-            if i == nb - 1:
+            if last:
                 dw_out(k).start()
-        dxa_in.wait()
+        dxa_in[i].wait()
+        if i == 0:
+            gp_in.start()
+            gy_in.start()
         dxs[i] = (dxa[i] + input_grad(w, dab)).astype(BF)
         dx_out(i).start()
         if i == 0:
@@ -337,11 +363,6 @@
             dxr_out.start()
             dw0_in.wait()
             dw0_out.start()
-            gp_in.wait()
-            gy_in.wait()
-            for c in range(NCH):
-                gn[c // 2, :, (c % 2) * CW:(c % 2 + 1) * CW] = gp[c].astype(F32) + gy[c].astype(F32)
-            gn_out.start()
     for i in range(nb):
         dx_out(i).wait()
     for k in range(3):
@@ -378,7 +399,7 @@
         vmem((nb, TB, D), BF), vmem((nb, TB, D), BF), vmem((3, HQ, D), BF), vmem((NB1 * TB, D), BF), vmem((nb, TB, D), F32),
         vmem((nb, TB, D), BF), vmem((3, TB, HQ), BF), vmem((3, 2, HS, D), F32), vmem((3, 2, HS, D), F32),
         vmem((NCH, HS, CW), BF), vmem((NCH, HS, CW), BF), vmem((3, HS, D), F32),
-        dma((nb,)), dma((nb,)), dma, dma((nb,)), dma((5,)), dma((nb,)), dma((3,)), dma((3,)),
+        dma((nb,)), dma((nb,)), dma((HQ // NT_COLS,)), dma((nb,)), dma((5,)), dma((nb,)), dma((3,)), dma((3,)),
     ]
     return pl.pallas_call(
         second_kernel,

time: 75.8 us -> 74 us (0.976)
  Pallas kernels: 74.8 us -> 73.1 us
    pallas_call x1, Pallas kernels: 21.5 us -> 20.4 us  [fused_step(): pl.pallas_call(second_kernel, out_shape=(sds((T, D), BF), sds((3, 4, HS,...]
where the time goes in v4:
time: 74 us; the launch traced here: 73.9 us
  Pallas kernels  73.1 us (99%)
  between operations  0.82 us (1%)
    pallas_call x1, Pallas kernels, fused_step(): pl.pallas_call(first_kernel, out_shape=(sds((NB1 * TB, D), BF), sds((nb *...  52.6 us
    pallas_call x1, Pallas kernels, fused_step(): pl.pallas_call(second_kernel, out_shape=(sds((T, D), BF), sds((3, 4, HS,...  20.4 us

profile of v4, /device:TPU:0, one launch (start us, length us, event | category | flops | bytes accessed | tf_op | source)
XLA Modules:
  0.0 73.9 jit_solution(13788932712905120882)
XLA Ops:
  0.6 52.6 %shard_map.85 = (bf16[2048,512]{1,0:T(8,128)(2,1)}, f32[2048,512]{1,0:T(8,128)}, f32[3,2,344,512]{3,2,1,0:T(8,128)}, f32[3,2,344,512]{3,2,1,0:T(8,128)}, bf16[3,...) custom-call(bf16[4096,512]{1,0:T(8,128)(2,1)} %x_hbm.3, ...), custom_call_target="tpu_custom_call" | custom-call | tf_op jit(solution)/shard_map/pallas_call | solution.py:390
  53.3 20.4 %shard_map.86 = (bf16[4096,512]{1,0:T(8,128)(2,1)}, f32[3,4,344,512]{3,2,1,0:T(8,128)}, f32[3,344,512]{2,1,0:T(8,128)}) custom-call(bf16[4096,512]{1,0:T(8,128)(2,1)} %x_hbm.3, bf16[4096,512]{1,0:T(8,128)(2,1)} %dy_hbm.3, bf16[2048,512]{1,0:T(8,128)(2,1)} %get-tuple-element.13.dxr_hbm, f32[2048,512]{1,0:T(8,128)} %get-tuple-element.14.dxa_hbm, ...), custom_call_target="tpu_custom_call" | custom-call | tf_op jit(solution)/shard_map/pallas_call | solution.py:404

commit v5 on v4

--- a/solution.py
+++ b/solution.py
@@ -155,18 +155,18 @@
     for m in range(3):
         wload(m).wait()
         a1(m).start()
-        a2(2 * m).start()
-        a2(2 * m + 1).start()
+    for j in range(NWP):
+        a2(j).start()
     for cp in xload(0):
         cp.start()
     for c in range(2):
         gload(c).start()
     for c in range(2):
         convert(c)
+    for m in range(3):
+        a1(m).wait_recv()
     for c in range(2):
         psend(c).start()
-    for m in range(3):
-        a1(m).wait_recv()
     for c in range(2, 5):
         gload(c).start()
     for i in range(1, NBLK):
@@ -236,11 +236,9 @@
 
     lax.fori_loop(0, NBLK, body, 0)
     dw0_out.start()
-    dxa_out.start()
     for j in range(NWP):
         a4(0, j, dp).wait_recv()
         a4(1, j, 1 - dp).wait_recv()
-    w_out.start()
 
     for i in range(NB1):
         rows = block_rows(i)
@@ -252,6 +250,8 @@
             actions(n + 1)
         if i == 0:
             dw0_out.wait()
+            dxa_out.start()
+            w_out.start()
         for k in range(3):
             weight_grad(k, x[rows, :], dy[rows, :], dab, dw, i == 0)
             if i == NB1 - 1:
@@ -316,53 +316,52 @@
     w_in(0).start()
     x_in[0].start()
     dy_in[0].start()
-    for t in range(1, tiles):
-        w_in(t).start()
     x_in[0].wait()
     dy_in[0].wait()
     for i in range(nb):
-        last = i == nb - 1
-        if i > 0:
+        first, last = i == 0, i == nb - 1
+        if not first:
             x_in[i].wait()
             dy_in[i].wait()
 
         def before(t):
-            if i == 0:
+            if first:
                 w_in(t).wait()
-                if t == tiles - 1:
+                if t == 0:
+                    for n in range(1, tiles):
+                        w_in(n).start()
+                if t == 1:
+                    dxa_in[0].start()
                     dwa_in.start()
-                    dxa_in[0].start()
+            elif last and t == tiles - 1:
+                dxr_in.wait()
+                dxr_out.start()
+                dw0_in.wait()
+                dw0_out.start()
 
         activations(x[i], dy[i], w, dab, before)
-        if i == 0:
-            dwa_in.wait()
         if not last:
             for cp in (x_in[i + 1], dy_in[i + 1], dxa_in[i + 1]):
                 cp.start()
-        if i == 0:
-            dxr_in.start()
-            dw0_in.start()
         if last:
             gp_in.wait()
             gy_in.wait()
             for c in range(NCH):
                 gn[c // 2, :, (c % 2) * CW:(c % 2 + 1) * CW] = gp[c].astype(F32) + gy[c].astype(F32)
             gn_out.start()
-        for k in range(3):
-            weight_grad(k, x[i], dy[i], dab, dw, False)
-            if last:
+            for k in range(3):
+                weight_grad(k, x[i], dy[i], dab, dw, False)
                 dw_out(k).start()
         dxa_in[i].wait()
-        if i == 0:
-            gp_in.start()
-            gy_in.start()
         dxs[i] = (dxa[i] + input_grad(w, dab)).astype(BF)
         dx_out(i).start()
-        if i == 0:
-            dxr_in.wait()
-            dxr_out.start()
-            dw0_in.wait()
-            dw0_out.start()
+        if first:
+            for cp in (dxr_in, dw0_in, gp_in, gy_in):
+                cp.start()
+            dwa_in.wait()
+        if not last:
+            for k in range(3):
+                weight_grad(k, x[i], dy[i], dab, dw, False)
     for i in range(nb):
         dx_out(i).wait()
     for k in range(3):

time: 74 us -> 73.1 us (0.988)
  Pallas kernels: 73.1 us -> 72.2 us
    pallas_call x1, Pallas kernels: 20.4 us -> 19.5 us  [fused_step(): pl.pallas_call(second_kernel, out_shape=(sds((T, D), BF), sds((3, 4, HS,...]
where the time goes in v5:
time: 73.1 us; the launch traced here: 73 us
  Pallas kernels  72.2 us (99%)
  between operations  0.82 us (1%)
    pallas_call x1, Pallas kernels, fused_step(): pl.pallas_call(first_kernel, out_shape=(sds((NB1 * TB, D), BF), sds((nb *...  52.6 us
    pallas_call x1, Pallas kernels, fused_step(): pl.pallas_call(second_kernel, out_shape=(sds((T, D), BF), sds((3, 4, HS,...  19.5 us

profile of v5, /device:TPU:0, one launch (start us, length us, event | category | flops | bytes accessed | tf_op | source)
XLA Modules:
  0.0 73.0 jit_solution(4126371004634479034)
XLA Ops:
  0.6 52.6 %shard_map.85 = (bf16[2048,512]{1,0:T(8,128)(2,1)}, f32[2048,512]{1,0:T(8,128)}, f32[3,2,344,512]{3,2,1,0:T(8,128)}, f32[3,2,344,512]{3,2,1,0:T(8,128)}, bf16[3,...) custom-call(bf16[4096,512]{1,0:T(8,128)(2,1)} %x_hbm.3, ...), custom_call_target="tpu_custom_call" | custom-call | tf_op jit(solution)/shard_map/pallas_call | solution.py:389
  53.3 19.5 %shard_map.86 = (bf16[4096,512]{1,0:T(8,128)(2,1)}, f32[3,4,344,512]{3,2,1,0:T(8,128)}, f32[3,344,512]{2,1,0:T(8,128)}) custom-call(bf16[4096,512]{1,0:T(8,128)(2,1)} %x_hbm.3, bf16[4096,512]{1,0:T(8,128)(2,1)} %dy_hbm.3, bf16[2048,512]{1,0:T(8,128)(2,1)} %get-tuple-element.13.dxr_hbm, f32[2048,512]{1,0:T(8,128)} %get-tuple-element.14.dxa_hbm, ...), custom_call_target="tpu_custom_call" | custom-call | tf_op jit(solution)/shard_map/pallas_call | solution.py:403

commit v6 on v5

--- a/solution.py
+++ b/solution.py
@@ -21,6 +21,7 @@
 NCH, CW = 6, 256
 NWP, WW = 6, 128
 NT_COLS, GATE_ROWS = 256, 64
+HB = TB // 2
 NB1 = 2
 
 NN = (((1,), (0,)), ((), ()))
@@ -58,8 +59,8 @@
             dab[0, rows, cols], dab[1, rows, cols], dab[2, rows, cols] = da, db, h
 
 
-def input_grad(w, dab):
-    return dot(dab[0], w[0], NN) + dot(dab[1], w[1], NN)
+def input_grad(w, dab, rows=slice(0, TB)):
+    return dot(dab[0, rows], w[0], NN) + dot(dab[1, rows], w[1], NN)
 
 
 def weight_grad(k, xb, dyb, dab, dw, fresh):
@@ -127,7 +128,7 @@
         return pltpu.make_async_copy(pk.at[c, f, row], gp_hbm.at[c], gp_sem.at[c])
 
     def dx_out(i):
-        return pltpu.make_async_copy(dxs.at[i % 2], dxr_hbm.at[block_rows(i)], dx_sem.at[i % 2])
+        return [pltpu.make_async_copy(dxs.at[i, pl.ds(h, HB)], dxr_hbm.at[pl.ds(i * TB + h, HB)], dx_sem.at[i, h // HB]) for h in (0, HB)]
 
     def dwa_out(k):
         return pltpu.make_async_copy(dw.at[k], dwa_hbm.at[k], dwa_sem.at[k])
@@ -256,8 +257,10 @@
             weight_grad(k, x[rows, :], dy[rows, :], dab, dw, i == 0)
             if i == NB1 - 1:
                 dwa_out(k).start()
-        dxs[i % 2] = (dxa[rows, :] + input_grad(wall.at[1], dab)).astype(BF)
-        dx_out(i).start()
+        for h, cp in zip((0, HB), dx_out(i)):
+            part = slice(h, h + HB)
+            dxs[i, part] = (dxa[i * TB + h:i * TB + h + HB, :] + input_grad(wall.at[1], dab, part)).astype(BF)
+            cp.start()
 
     for m in range(3):
         a1(m).wait_send()
@@ -272,7 +275,8 @@
         ysend(c).wait_send()
         gp_out(c).wait()
     for i in range(NB1):
-        dx_out(i).wait()
+        for cp in dx_out(i):
+            cp.wait()
     dxa_out.wait()
     w_out.wait()
     for k in range(3):
@@ -295,7 +299,7 @@
                 pltpu.make_async_copy(dxa_hbm.at[block_rows(i)], dxa.at[i], dxa_sem.at[i]))
 
     def dx_out(i):
-        return pltpu.make_async_copy(dxs.at[i], dx_hbm.at[block_rows(NB1 + i)], dx_sem.at[i])
+        return [pltpu.make_async_copy(dxs.at[i, pl.ds(h, HB)], dx_hbm.at[pl.ds((NB1 + i) * TB + h, HB)], dx_sem.at[i, h // HB]) for h in (0, HB)]
 
     def dw_out(k):
         return pltpu.make_async_copy(dw.at[k], dwt_hbm.at[k, pl.ds(2 * (1 - row), 2)], dw_sem.at[k])
@@ -353,8 +357,10 @@
                 weight_grad(k, x[i], dy[i], dab, dw, False)
                 dw_out(k).start()
         dxa_in[i].wait()
-        dxs[i] = (dxa[i] + input_grad(w, dab)).astype(BF)
-        dx_out(i).start()
+        for h, cp in zip((0, HB), dx_out(i)):
+            part = slice(h, h + HB)
+            dxs[i, part] = (dxa[i, part] + input_grad(w, dab, part)).astype(BF)
+            cp.start()
         if first:
             for cp in (dxr_in, dw0_in, gp_in, gy_in):
                 cp.start()
@@ -363,7 +369,8 @@
             for k in range(3):
                 weight_grad(k, x[i], dy[i], dab, dw, False)
     for i in range(nb):
-        dx_out(i).wait()
+        for cp in dx_out(i):
+            cp.wait()
     for k in range(3):
         dw_out(k).wait()
     for cp in (dxr_out, dw0_out, gn_out):
@@ -378,9 +385,9 @@
     nb = NBLK - NB1
     scratch = [
         vmem((T, D), BF), vmem((T, D), BF), vmem((2, 3, HQ, D), BF),
-        vmem((T, D), F32), vmem((2, TB, D), BF), vmem((3, TB, HQ), BF), vmem((3, 2, HS, D), F32),
+        vmem((T, D), F32), vmem((NB1, TB, D), BF), vmem((3, TB, HQ), BF), vmem((3, 2, HS, D), F32),
         vmem((3, 4, HS, CW), F32), vmem((NCH, 2, 2, HS, CW), BF), vmem((NCH, 2, HS, CW), BF), vmem((NCH, HS, CW), BF),
-        dma((NBLK,)), dma((NBLK,)), dma((3,)), dma((3,)), dma((2,)), dma, dma, dma((3,)), dma, dma((NCH,)),
+        dma((NBLK,)), dma((NBLK,)), dma((3,)), dma((3,)), dma((NB1, 2)), dma, dma, dma((3,)), dma, dma((NCH,)),
         dma((3,)), dma((3,)), dma((NWP,)), dma((NWP,)), dma((NWP,)), dma((NWP,)), dma((2, NWP)), dma((2, NWP)),
         dma((NCH,)), dma((NCH,)), dma((NCH,)), dma((NCH,)), dma((NCH,)), dma((NCH,)),
     ]
@@ -398,7 +405,7 @@
         vmem((nb, TB, D), BF), vmem((nb, TB, D), BF), vmem((3, HQ, D), BF), vmem((NB1 * TB, D), BF), vmem((nb, TB, D), F32),
         vmem((nb, TB, D), BF), vmem((3, TB, HQ), BF), vmem((3, 2, HS, D), F32), vmem((3, 2, HS, D), F32),
         vmem((NCH, HS, CW), BF), vmem((NCH, HS, CW), BF), vmem((3, HS, D), F32),
-        dma((nb,)), dma((nb,)), dma((HQ // NT_COLS,)), dma((nb,)), dma((5,)), dma((nb,)), dma((3,)), dma((3,)),
+        dma((nb,)), dma((nb,)), dma((HQ // NT_COLS,)), dma((nb,)), dma((5,)), dma((nb, 2)), dma((3,)), dma((3,)),
     ]
     return pl.pallas_call(
         second_kernel,

time: 73.1 us -> 72.8 us (level)
  no operation moved by 1% of the time
where the time goes in v6:
time: 72.8 us; the launch traced here: 72.7 us
  Pallas kernels  71.9 us (99%)
  between operations  0.82 us (1%)
    pallas_call x1, Pallas kernels, fused_step(): pl.pallas_call(first_kernel, out_shape=(sds((NB1 * TB, D), BF), sds((nb *...  52.4 us
    pallas_call x1, Pallas kernels, fused_step(): pl.pallas_call(second_kernel, out_shape=(sds((T, D), BF), sds((3, 4, HS,...  19.4 us

profile of v6, /device:TPU:0, one launch (start us, length us, event | category | flops | bytes accessed | tf_op | source)
XLA Modules:
  0.0 72.7 jit_solution(13610385912389480827)
XLA Ops:
  0.6 52.4 %shard_map.85 = (bf16[2048,512]{1,0:T(8,128)(2,1)}, f32[2048,512]{1,0:T(8,128)}, f32[3,2,344,512]{3,2,1,0:T(8,128)}, f32[3,2,344,512]{3,2,1,0:T(8,128)}, bf16[3,...) custom-call(bf16[4096,512]{1,0:T(8,128)(2,1)} %x_hbm.3, ...), custom_call_target="tpu_custom_call" | custom-call | tf_op jit(solution)/shard_map/pallas_call | solution.py:396
  53.1 19.4 %shard_map.86 = (bf16[4096,512]{1,0:T(8,128)(2,1)}, f32[3,4,344,512]{3,2,1,0:T(8,128)}, f32[3,344,512]{2,1,0:T(8,128)}) custom-call(bf16[4096,512]{1,0:T(8,128)(2,1)} %x_hbm.3, bf16[4096,512]{1,0:T(8,128)(2,1)} %dy_hbm.3, bf16[2048,512]{1,0:T(8,128)(2,1)} %get-tuple-element.13.dxr_hbm, f32[2048,512]{1,0:T(8,128)} %get-tuple-element.14.dxa_hbm, ...), custom_call_target="tpu_custom_call" | custom-call | tf_op jit(solution)/shard_map/pallas_call | solution.py:410
